TPU v7x, 32 devices: a whole 2x2x4 slice. The times are simulated.
32 devices in a mesh: freq: 4 (over y, x), space: 8 (over z, core).
Axes of the slice: x: 2, y: 2, z: 4, core: 2. Of those that a mesh axis runs over, the one named last changes fastest.
Arguments:
- snapshots: float32 [2, 256, 3, 4096], P(None, 'freq', None, 'space'), may hold values from -6 to 6
- mean_field: float32 [3, 4096], P(None, 'space'), may hold values from -3 to 3
- weights: float32 [3, 4096], P(None, 'space'), may hold values from 0.25 to 4
- rates: float32 [128], P('freq'), may hold values from 0.2 to 0.8
- modes: float32 [128, 2, 16, 3, 4096], P('freq', None, None, None, 'space'), may hold values from -6 to 6
Outputs:
- modes_out: float32 [128, 2, 16, 3, 4096], P('freq', None, None, None, 'space')
- coefficients: float32 [2, 128, 2, 16], P(None, 'freq')
All inputs are finite; a program needn't handle non-finite values.
Results may differ from a plain program's by a relative error of at most 0.00024.
Values sent between devices are 32-bit elements; how exact they have to be, the bound alone decides.
No kernel may reach another device: no remote copies, remote signals or barrier semaphores. Data moves between devices by JAX's collectives and lax.ppermute only.
A program may use at most 64 MiB of HBM per device.

v0:
```python
import math

import jax
import jax.numpy as jnp
from jax import lax
from jax.experimental import pallas as pl
from jax.experimental.pallas import tpu as pltpu
from jax.sharding import PartitionSpec as P

EPS = 1e-06


def spectral_table(freq_ids, time_ids, length):
    phase = freq_ids[:, None] * time_ids[None, :] % length
    angle = 2.0 * math.pi / length * phase.astype(jnp.float32)
    window = 0.5 - 0.5 * jnp.cos(2.0 * math.pi / length * time_ids.astype(jnp.float32))
    weight_row = window / math.sqrt(3.0 * length / 8.0)
    return jnp.concatenate(
        (jnp.cos(angle) * weight_row[None], -jnp.sin(angle) * weight_row[None]), axis=0
    )


def split(value):
    high = value.astype(jnp.bfloat16)
    low = (value - high.astype(jnp.float32)).astype(jnp.bfloat16)
    return high, low


def nt_dot(left, right):
    return lax.dot_general(
        left, right, (((1,), (1,)), ((), ())), preferred_element_type=jnp.float32
    )


def gram_kernel(w_ref, m_ref, g_ref):
    fields = m_ref.shape[2]
    kk = m_ref.shape[3]

    def one(i, carry):
        total = jnp.zeros((2 * kk, 2 * kk), jnp.float32)
        for c in range(fields):
            root = jnp.sqrt(w_ref[c])
            both = jnp.concatenate((m_ref[i, 0, c] * root, m_ref[i, 1, c] * root), axis=0)
            high, low = split(both)
            total += nt_dot(high, high) + nt_dot(low, high) + nt_dot(high, low)
        g_ref[i, :, :kk] = total[:kk, :kk] + total[kk:, kk:]
        g_ref[i, :, kk:] = total[:kk, kk:] - total[kk:, :kk]
        return carry

    lax.fori_loop(0, m_ref.shape[0], one, 0)


def lane_sum(value):
    return jnp.sum(value, axis=1, keepdims=True)


def project_kernel(w_ref, q_ref, m_ref, p_ref):
    step = pl.program_id(0)
    per_step = m_ref.shape[0]
    fields = m_ref.shape[2]
    kk = m_ref.shape[3]
    count = q_ref.shape[3]
    lanes = p_ref.shape[1]

    @pl.when(step == 0)
    def _():
        p_ref[...] = jnp.zeros_like(p_ref)

    lane = lax.broadcasted_iota(jnp.int32, (kk, lanes), 1)
    lane_row = lax.broadcasted_iota(jnp.int32, (1, lanes), 1)

    def one(i, carry):
        f = step * per_step + i
        accs = [0.0] * 4
        rows = [0.0] * 4
        for c in range(fields):
            mr = m_ref[i, 0, c]
            mi = m_ref[i, 1, c]
            w = w_ref[c]
            qs = [q_ref[b, c, s, pl.ds(f, 1), :] for b in range(2) for s in range(2)]
            wq = [w * q for q in qs]
            for b in range(2):
                accs[2 * b] += mr * wq[2 * b] + mi * wq[2 * b + 1]
                accs[2 * b + 1] += mr * wq[2 * b + 1] - mi * wq[2 * b]
            rows[0] += wq[0] * qs[0] + wq[1] * qs[1]
            rows[1] += wq[2] * qs[2] + wq[3] * qs[3]
            rows[2] += wq[0] * qs[2] + wq[1] * qs[3]
            rows[3] += wq[0] * qs[3] - wq[1] * qs[2]
        tile = p_ref[:kk]
        row = p_ref[kk : kk + 1]
        for j in range(4):
            spot = j * count + f
            tile = jnp.where(lane == spot, lane_sum(accs[j]), tile)
            row = jnp.where(lane_row == spot, lane_sum(rows[j]), row)
        p_ref[:kk] = tile
        p_ref[kk : kk + 1] = row
        return carry

    lax.fori_loop(0, per_step, one, 0)


def small_math(g_ref, p_ref, rate_ref, coef_ref, tab_ref, point_count):
    kk = g_ref.shape[1]
    count = g_ref.shape[3]
    root = math.sqrt(point_count)
    total = p_ref[0]
    for s in range(1, p_ref.shape[0]):
        total = total + p_ref[s]
    part = [total[:kk, j * count : (j + 1) * count] for j in range(4)]
    row = [total[kk : kk + 1, j * count : (j + 1) * count] for j in range(4)]
    p0r, p0i, p1r, p1i = part
    e00, e11, xr, xi = row
    rate = rate_ref[...]

    def sum_k(value):
        return jnp.sum(value, axis=0, keepdims=True)

    def times_gram(hr, hi):
        vr = jnp.zeros((kk, count), jnp.float32)
        vi = jnp.zeros((kk, count), jnp.float32)
        for l in range(kk):
            gr = g_ref[0, l]
            gi = g_ref[1, l]
            ar = hr[l : l + 1]
            ai = hi[l : l + 1]
            vr += gr * ar - gi * ai
            vi += gr * ai + gi * ar
        return vr, vi

    sub = lax.broadcasted_iota(jnp.int32, (kk, count), 0)
    diag = jnp.zeros((kk, count), jnp.float32)
    for l in range(kk):
        diag = jnp.where(sub == l, g_ref[0, l], diag)

    a0r = p0r / root
    a0i = p0i / root
    gain0 = rate / jnp.sqrt(e00 / point_count + EPS)
    cr = gain0 * a0r
    ci = -gain0 * a0i
    br = a0r / root
    bi = a0i / root
    vr, vi = times_gram(br, bi)
    sr = p0r - vr
    si = p0i - vi
    t0 = e00 - sum_k(br * p0r + bi * p0i) - sum_k(sr * br + si * bi)
    t0 = jnp.maximum(t0, 0.0)
    n0 = diag + 2.0 * (cr * sr - ci * si) + (cr * cr + ci * ci) * t0
    n0 = jnp.maximum(n0, 0.0) / point_count
    d0 = 1.0 / jnp.sqrt(n0 + EPS)
    yr = xr - sum_k(br * p1r + bi * p1i)
    yi = xi - sum_k(br * p1i - bi * p1r)
    u1r = d0 * (p1r + cr * yr + ci * yi)
    u1i = d0 * (p1i + cr * yi - ci * yr)
    a1r = u1r / root
    a1i = u1i / root
    gain1 = rate / jnp.sqrt(e11 / point_count + EPS)
    er = gain1 * a1r
    ei = -gain1 * a1i
    b1r = a1r / root
    b1i = a1i / root
    hr = d0 * b1r
    hi = d0 * b1i
    bigr = sum_k(cr * hr - ci * hi)
    bigi = sum_k(cr * hi + ci * hr)
    zr = sum_k(sr * hr + si * hi)
    zi = sum_k(sr * hi - si * hr)
    vr, vi = times_gram(hr, hi)
    kr = zr + t0 * bigr
    ki = zi + t0 * bigi
    s1r = u1r - d0 * (vr + sr * bigr - si * bigi + cr * kr + ci * ki)
    s1i = u1i - d0 * (vi + sr * bigi + si * bigr + cr * ki - ci * kr)
    t1 = e11 - sum_k(b1r * u1r + b1i * u1i) - sum_k(s1r * b1r + s1i * b1i)
    t1 = jnp.maximum(t1, 0.0)
    n1 = d0 * d0 * n0 * point_count + 2.0 * (er * s1r - ei * s1i) + (er * er + ei * ei) * t1
    n1 = jnp.maximum(n1, 0.0) / point_count
    d1 = 1.0 / jnp.sqrt(n1 + EPS)
    both = d0 * d1
    coef_ref[0, 0] = a0r
    coef_ref[0, 1] = a0i
    coef_ref[1, 0] = a1r
    coef_ref[1, 1] = a1i
    wide = jnp.zeros((kk, count), jnp.float32)
    for n, value in enumerate(
        (br, bi, hr, hi, both, both * cr, both * ci, d1 * er, d1 * ei, wide + bigr, wide + bigi)
    ):
        tab_ref[n] = value


def update_kernel(g_ref, p_ref, rate_ref, q_ref, m_ref, out_ref, coef_ref, tab_ref, *, point_count):
    step = pl.program_id(0)
    per_step = m_ref.shape[0]
    fields = m_ref.shape[2]
    kk = m_ref.shape[3]
    count = q_ref.shape[3]

    @pl.when(step == 0)
    def _():
        small_math(g_ref, p_ref, rate_ref, coef_ref, tab_ref, point_count)

    lane = lax.broadcasted_iota(jnp.int32, (kk, count), 1)

    def one(i, carry):
        f = step * per_step + i
        here = lane == f
        cols = [lane_sum(jnp.where(here, tab_ref[n], 0.0)) for n in range(tab_ref.shape[0])]
        br, bi, hr, hi, ad, cr, ci, er, ei = cols[:9]
        bigr = cols[9][:1]
        bigi = cols[10][:1]
        for c in range(fields):
            mr = m_ref[i, 0, c]
            mi = m_ref[i, 1, c]
            q0r, q0i, q1r, q1i = [
                q_ref[b, c, s, pl.ds(f, 1), :] for b in range(2) for s in range(2)
            ]
            r0r = q0r - jnp.sum(br * mr - bi * mi, axis=0, keepdims=True)
            r0i = q0i - jnp.sum(br * mi + bi * mr, axis=0, keepdims=True)
            r1r = q1r - jnp.sum(hr * mr - hi * mi, axis=0, keepdims=True)
            r1i = q1i - jnp.sum(hr * mi + hi * mr, axis=0, keepdims=True)
            r1r = r1r - (bigr * r0r - bigi * r0i)
            r1i = r1i - (bigr * r0i + bigi * r0r)
            out_ref[i, 0, c] = ad * mr + (cr * r0r - ci * r0i) + (er * r1r - ei * r1i)
            out_ref[i, 1, c] = ad * mi + (cr * r0i + ci * r0r) + (er * r1i + ei * r1r)
        return carry

    lax.fori_loop(0, per_step, one, 0)


def share(value, axis):
    size = lax.axis_size(axis)
    return lax.all_to_all(
        jnp.broadcast_to(value[None], (size,) + value.shape), axis, 0, 0, tiled=True
    )


def per_device(snapshots, mean_field, weights, rates, modes):
    freq_count = lax.axis_size("freq")
    blocks, quarter, fields, points = snapshots.shape
    assert blocks == 2
    length = quarter * freq_count
    point_count = fields * points * lax.axis_size("space")
    count, _, kk = modes.shape[:3]
    per_step = math.gcd(count, 4)
    steps = count // per_step
    me = lax.axis_index("freq")
    snaps = snapshots.transpose(0, 2, 1, 3)
    ms = modes.transpose(0, 1, 3, 2, 4)
    w3 = weights[:, None, :]

    moved = [snaps]
    for m in range(1, freq_count):
        if freq_count & (freq_count - 1) == 0:
            pairs = [(i, i ^ m) for i in range(freq_count)]
        else:
            pairs = [(i, (i + m) % freq_count) for i in range(freq_count)]
        moved.append(lax.ppermute(snaps, "freq", pairs))

    m_spec = pl.BlockSpec((per_step, 2, fields, kk, points), lambda s: (s, 0, 0, 0, 0))
    w_spec = pl.BlockSpec((fields, 1, points), lambda s: (0, 0, 0))
    q_spec = pl.BlockSpec((blocks, fields, 2, count, points), lambda s: (0, 0, 0, 0, 0))

    gram = pl.pallas_call(
        gram_kernel,
        grid=(steps,),
        in_specs=[w_spec, m_spec],
        out_specs=pl.BlockSpec((per_step, kk, 2 * kk), lambda s: (s, 0, 0)),
        out_shape=jax.ShapeDtypeStruct((count, kk, 2 * kk), jnp.float32),
        name="gram",
    )(w3, ms)
    gram = jnp.sum(share(gram.reshape(count * kk * 2 * kk // 128, 128), "space"), axis=0)
    gram = gram.reshape(count, kk, 2, kk).transpose(2, 3, 1, 0)

    freq_ids = me * count + jnp.arange(count, dtype=jnp.int32)
    spectra = 0.0
    for m in range(freq_count):
        if freq_count & (freq_count - 1) == 0:
            source = me ^ m
        else:
            source = (me - m) % freq_count
        times = source * quarter + jnp.arange(quarter, dtype=jnp.int32)
        table = spectral_table(freq_ids, times, length)
        spectra = spectra + jnp.einsum(
            "rt,bctp->bcrp",
            table,
            moved[m] - mean_field[None, :, None, :],
            precision=lax.Precision.HIGHEST,
        )
    spectra = spectra.reshape(blocks, fields, 2, count, points)

    rows = -(-(kk + 1) // 8) * 8
    lanes = 4 * count
    prods = pl.pallas_call(
        project_kernel,
        grid=(steps,),
        in_specs=[w_spec, q_spec, m_spec],
        out_specs=pl.BlockSpec((rows, lanes), lambda s: (0, 0)),
        out_shape=jax.ShapeDtypeStruct((rows, lanes), jnp.float32),
        name="project",
    )(w3, spectra, ms)
    prods = share(prods, "space")

    def full(shape):
        return pl.BlockSpec(shape, lambda s: (0,) * len(shape))

    out, coefs = pl.pallas_call(
        lambda *refs: update_kernel(*refs, point_count=point_count),
        grid=(steps,),
        in_specs=[full(gram.shape), full(prods.shape), full((1, count)), q_spec, m_spec],
        out_specs=[m_spec, full((blocks, 2, kk, count))],
        out_shape=[
            jax.ShapeDtypeStruct(ms.shape, jnp.float32),
            jax.ShapeDtypeStruct((blocks, 2, kk, count), jnp.float32),
        ],
        scratch_shapes=[pltpu.VMEM((11, kk, count), jnp.float32)],
        name="update",
    )(gram, prods, rates[None], spectra, ms)
    return out.transpose(0, 1, 3, 2, 4), coefs.transpose(0, 3, 1, 2)


def solution(mesh):
    return jax.shard_map(
        per_device,
        mesh=mesh,
        in_specs=(
            P(None, "freq", None, "space"),
            P(None, "space"),
            P(None, "space"),
            P("freq"),
            P("freq", None, None, None, "space"),
        ),
        out_specs=(P("freq", None, None, None, "space"), P(None, "freq", None, None)),
        check_vma=False,
    )
```

profile of v0, /device:TPU:0, one launch (start us, length us, event | category | flops | bytes accessed | tf_op | source)
XLA Modules:
  0.0 79.6 jit_solution(7077008459608643806)
XLA Ops:
  0.6 0.0 copy-start
  0.6 0.0 copy-start.2
  0.6 3.1 %collective-permute-start.1 = (f32[2,3,64,512]{3,2,1,0:T(8,128)}, f32[2,3,64,512]{3,2,1,0:T(8,128)S(1)}, u32[]{:S(2)}, u32[]{:S(2)}) collective-permute-start(f32[2,3,64,512]{3,2,1,0:T(8,128)} %bitcast.39), channel_id=1, source_target_pairs={{0,16},{8,24},{16,0},{24,8},{1,17},{9,25},{17,1},{25,9},{2,18},{10... | collective-permute-start | bytes 2359304 | tf_op jit(solution)/shard_map/ppermute | solution.py:255
  3.7 1.5 %collective-permute-start = (f32[2,3,64,512]{3,2,1,0:T(8,128)}, f32[2,3,64,512]{3,2,1,0:T(8,128)}, u32[]{:S(2)}, u32[]{:S(2)}) collective-permute-start(f32[2,3,64,512]{3,2,1,0:T(8,128)} %bitcast.40), channel_id=1, source_target_pairs={{0,8},{8,0},{16,24},{24,16},{1,9},{9,1},{17,25},{25,17},{2,10},{10... | collective-permute-start | bytes 2359304 | tf_op jit(solution)/shard_map/ppermute | solution.py:255
  5.2 0.0 collective-permute-start.2
  5.3 1.3 %broadcast_in_dim.10.w_ref = f32[3,1,512]{2,1,0:T(1,128)} reshape(f32[3,512]{1,0:T(4,128)} %param.7) | data formatting | bytes 12288 | tf_op jit(solution)/shard_map/broadcast_in_dim | solution.py:247
  6.5 11.4 %gram.1 = f32[32,16,32]{2,1,0:T(8,128)} custom-call(f32[3,1,512]{2,1,0:T(1,128)} %broadcast_in_dim.10.w_ref, f32[32,2,3,16,512]{4,3,2,1,0:T(8,128)} %bitcast.33), custom_call_target="tpu_custom_call" | custom-call | tf_op jit(solution)/shard_map/gram/pallas_call | solution.py:261
  17.9 1.1 %broadcast_in_dim.11 = f32[128,128]{1,0:T(8,128)S(1)} reshape(f32[32,16,32]{2,1,0:T(8,128)} %gram.1) | data formatting | bytes 131072 | tf_op jit(solution)/shard_map/broadcast_in_dim | solution.py:231
  19.0 0.8 %broadcast_in_dim.12 = f32[8,128,128]{2,1,0:T(8,128)} broadcast(f32[128,128]{1,0:T(8,128)S(1)} %broadcast_in_dim.11), dimensions={1,2} | broadcast | bytes 589824 | tf_op jit(solution)/shard_map/broadcast_in_dim | solution.py:231
  19.8 5.3 %all-to-all-start = ((f32[8,128,128]{2,1,0:T(8,128)}), f32[8,128,128]{2,1,0:T(8,128)S(1)}, u32[]{:S(2)}, u32[]{:S(2)}) async-start(f32[8,128,128]{2,1,0:T(8,128)} %broadcast_in_dim.12), calls=%async_computation | async-start | bytes 1048576 | tf_op jit(solution)/shard_map/all_to_all | solution.py:230
  25.1 0.1 subtract_multiply_fusion.2
  25.2 0.1 subtract_multiply_fusion
  25.3 0.4 cosine_multiply_fusion.1
  25.6 0.0 copy-done
  25.6 0.0 copy-done.2
  25.6 0.9 %fusion.5 = f32[2,3,512,64]{2,3,1,0:T(8,128)S(1)} fusion(f32[3,512]{1,0:T(4,128)S(1)} %copy-done.2, f32[32,64]{1,0:T(8,128)S(1)} %get-tuple-element.18, f32[32,64]{1,0:T(8,128)S(1)} %get-tuple-element.19, f32[2,64,3,512]{3,1,2,0:T(8,128)S(1)} %copy-done), kind=kOutput, calls=%fused_computation.7 | convolution fusion | flops 151195648 | bytes 1595392 | tf_op jit(solution)/shard_map/rt,bctp->bcrp/dot_general | solution.py:281
  26.6 13.0 %collective-permute-done.2 = f32[2,3,64,512]{3,2,1,0:T(8,128)S(1)} collective-permute-done((f32[2,3,64,512]{3,2,1,0:T(8,128)}, f32[2,3,64,512]{3,2,1,0:T(8,128)S(1)}, u32[]{:S(2)}, u32[]{:S(2)}) %collective-permute-start.2) | collective-permute-done | bytes 786464 | tf_op jit(solution)/shard_map/ppermute | solution.py:255
  39.6 0.9 %fusion.1 = f32[2,3,512,64]{2,3,1,0:T(8,128)S(1)} fusion(f32[2,3,64,512]{3,2,1,0:T(8,128)S(1)} %collective-permute-done.2, f32[3,512]{1,0:T(4,128)S(1)} %copy-done.2, f32[32,64]{1,0:T(8,128)S(1)} %get-tuple-element.16, f32[32,64]{1,0:T(8,128)S(1)} %get-tuple-element.17), kind=kOutput, calls=%fused_computation.3 | convolution fusion | flops 151195648 | bytes 1595392 | tf_op jit(solution)/shard_map/rt,bctp->bcrp/dot_general | solution.py:281
  40.5 0.0 collective-permute-done
  40.5 2.0 %convolution_add_fusion.1 = f32[2,3,512,64]{2,3,1,0:T(8,128)S(1)} fusion(f32[2,3,512,64]{2,3,1,0:T(8,128)S(1)} %fusion.5, f32[2,3,64,512]{3,2,1,0:T(8,128)} %collective-permute-done, f32[3,512]{1,0:T(4,128)S(1)} %copy-done.2, f32[32,64]{1,0:T(8,128)S(1)} %get-tuple-element.14, f32[32,64]{1,0:T(8,128)S(1)} %get-tuple-element.15), kind=kOutput, calls=%fused_computation.1 | convolution fusion | flops 151392256 | bytes 2381824 | tf_op jit(solution)/shard_map/rt,bctp->bcrp/dot_general | solution.py:281
  42.5 0.0 collective-permute-done.1
  42.6 1.9 %fusion = f32[2,3,512,64]{2,3,1,0:T(8,128)} fusion(f32[2,3,512,64]{2,3,1,0:T(8,128)S(1)} %fusion.1, f32[2,3,512,64]{2,3,1,0:T(8,128)S(1)} %convolution_add_fusion.1, f32[2,3,64,512]{3,2,1,0:T(8,128)S(1)} %collective-permute-done.1, f32[3,512]{1,0:T(4,128)S(1)} %copy-done.2, f32[32,64]{1,0:T(8,128)S(1)} %get-tuple-element.7, f32[32,64]{1,0:T(8,128)S(1)} %get-tuple-element.6), kind=kOutput, calls=%fused_computation.2 | convolution fusion | flops 151588864 | bytes 3168256 | tf_op jit(solution)/shard_map/rt,bctp->bcrp/dot_general | solution.py:281
  44.4 8.8 %project.1 = f32[24,128]{1,0:T(8,128)} custom-call(f32[3,1,512]{2,1,0:T(1,128)} %broadcast_in_dim.10.w_ref, f32[2,3,2,32,512]{4,3,2,1,0:T(8,128)} %bitcast.36, f32[32,2,3,16,512]{4,3,2,1,0:T(8,128)} %bitcast.34), custom_call_target="tpu_custom_call" | custom-call | tf_op jit(solution)/shard_map/project/pallas_call | solution.py:291
  53.3 0.0 all-to-all-done
  53.3 1.4 %broadcast_in_dim.13 = f32[8,24,128]{2,1,0:T(8,128)} broadcast(f32[24,128]{1,0:T(8,128)} %project.1), dimensions={1,2} | broadcast | bytes 110592 | tf_op jit(solution)/shard_map/broadcast_in_dim | solution.py:231
  54.6 5.0 %all-to-all-start.1 = ((f32[8,24,128]{2,1,0:T(8,128)}), f32[8,24,128]{2,1,0:T(8,128)S(1)}, u32[]{:S(2)}, u32[]{:S(2)}) async-start(f32[8,24,128]{2,1,0:T(8,128)} %broadcast_in_dim.13), calls=%async_computation.1 | async-start | bytes 196608 | tf_op jit(solution)/shard_map/all_to_all | solution.py:230
  59.7 0.7 reshape.65
  60.4 1.1 %copy.8 = f32[32,16,2,16]{0,1,3,2:T(8,128)} copy(f32[32,16,2,16]{3,2,1,0:T(2,128)S(1)} %reshape.65) | data formatting | bytes 131072 | tf_op jit(solution)/shard_map/reshape | solution.py:270
  61.5 4.5 %all-to-all-done.1.refs_1_ = f32[8,24,128]{2,1,0:T(8,128)S(1)} async-done(((f32[8,24,128]{2,1,0:T(8,128)}), f32[8,24,128]{2,1,0:T(8,128)S(1)}, u32[]{:S(2)}, u32[]{:S(2)}) %all-to-all-start.1) | async-done | bytes 98336 | tf_op jit(solution)/shard_map/all_to_all | solution.py:230
  66.0 0.0 copy-start.1
  66.0 0.6 copy-done.1
  66.6 13.0 %update.1 = (f32[32,2,3,16,512]{4,3,2,1,0:T(8,128)}, f32[2,2,16,32]{3,2,1,0:T(8,128)}) custom-call(f32[2,16,16,32]{3,2,1,0:T(8,128)} %bitcast.38, f32[8,24,128]{2,1,0:T(8,128)} %copy-done.1, f32[1,32]{1,0:T(1,128)} %bitcast.42, f32[2,3,2,32,512]{4,3,2,1,0:T(8,128)} %bitcast.37, f32[32,2,3,16,512]{4,3,2,1,0:T(8,128)} %bitcast.35), custom_call_target="tpu_custom_call" | custom-call | tf_op jit(solution)/shard_map/update/pallas_call | solution.py:304
  (4 shorter events, 0.0 us)
Async XLA Ops:
  0.6 25.0 %copy-start = (f32[2,64,3,512]{3,1,2,0:T(8,128)S(1)}, f32[2,64,3,512]{3,1,2,0:T(8,128)}, u32[]{:S(2)}) copy-start(f32[2,64,3,512]{3,1,2,0:T(8,128)} %param.5) | copy-start | bytes 2359300
  0.6 25.0 %copy-start.2 = (f32[3,512]{1,0:T(4,128)S(1)}, f32[3,512]{1,0:T(4,128)}, u32[]{:S(2)}) copy-start(f32[3,512]{1,0:T(4,128)} %param.6) | copy-start | bytes 18436
  0.6 41.9 %collective-permute-start.1 = (f32[2,3,64,512]{3,2,1,0:T(8,128)}, f32[2,3,64,512]{3,2,1,0:T(8,128)S(1)}, u32[]{:S(2)}, u32[]{:S(2)}) collective-permute-start(f32[2,3,64,512]{3,2,1,0:T(8,128)} %bitcast.39), channel_id=1, source_target_pairs={{0,16},{8,24},{16,0},{24,8},{1,17},{9,25},{17,1},{25,9},{2,18},{10... | collective-permute-start | bytes 2359304 | tf_op jit(solution)/shard_map/ppermute | solution.py:255
  3.7 36.8 %collective-permute-start = (f32[2,3,64,512]{3,2,1,0:T(8,128)}, f32[2,3,64,512]{3,2,1,0:T(8,128)}, u32[]{:S(2)}, u32[]{:S(2)}) collective-permute-start(f32[2,3,64,512]{3,2,1,0:T(8,128)} %bitcast.40), channel_id=1, source_target_pairs={{0,8},{8,0},{16,24},{24,16},{1,9},{9,1},{17,25},{25,17},{2,10},{10... | collective-permute-start | bytes 2359304 | tf_op jit(solution)/shard_map/ppermute | solution.py:255
  5.2 34.4 %collective-permute-start.2 = (f32[2,3,64,512]{3,2,1,0:T(8,128)}, f32[2,3,64,512]{3,2,1,0:T(8,128)S(1)}, u32[]{:S(2)}, u32[]{:S(2)}) collective-permute-start(f32[2,3,64,512]{3,2,1,0:T(8,128)} %bitcast.41), channel_id=1, source_target_pairs={{0,24},{8,16},{16,8},{24,0},{1,25},{9,17},{17,9},{25,1},{2,26},{10... | collective-permute-start | bytes 2359304 | tf_op jit(solution)/shard_map/ppermute | solution.py:255
  19.8 33.5 %all-to-all-start = ((f32[8,128,128]{2,1,0:T(8,128)}), f32[8,128,128]{2,1,0:T(8,128)S(1)}, u32[]{:S(2)}, u32[]{:S(2)}) async-start(f32[8,128,128]{2,1,0:T(8,128)} %broadcast_in_dim.12), calls=%async_computation | async-start | bytes 1048576 | tf_op jit(solution)/shard_map/all_to_all | solution.py:230
  54.6 11.3 %all-to-all-start.1 = ((f32[8,24,128]{2,1,0:T(8,128)}), f32[8,24,128]{2,1,0:T(8,128)S(1)}, u32[]{:S(2)}, u32[]{:S(2)}) async-start(f32[8,24,128]{2,1,0:T(8,128)} %broadcast_in_dim.13), calls=%async_computation.1 | async-start | bytes 196608 | tf_op jit(solution)/shard_map/all_to_all | solution.py:230
  66.0 0.6 copy-start.1
where the time goes:
time: 80.5 us; the launch traced here: 79.6 us
  Pallas kernels  33.2 us (41%)
  waiting for transfers between devices  17.5 us (22%)
  starting transfers between devices  14.9 us (19%)
  local copies, waits for them, and re-layouts  6.98 us (9%)
  matrix products  5.75 us (7%)
    pallas_call x1, Pallas kernels, per_device(): pl.pallas_call(lambda *refs: update_kernel(*refs, point_count=point_count...  13 us
    ppermute x3, waiting for transfers between devices, per_device(): moved.append(lax.ppermute(snaps, 'freq', pairs))  13 us
    pallas_call x1, Pallas kernels, per_device(): pl.pallas_call(gram_kernel, grid=(steps,), in_specs=[w_spec, m_spec], out...  11.4 us
    all_to_all x2, starting transfers between devices, share(): lax.all_to_all(jnp.broadcast_to(value[None], (size,) + value.shape), axis...  10.3 us
    pallas_call x1, Pallas kernels, per_device(): pl.pallas_call(project_kernel, grid=(steps,), in_specs=[w_spec, q_spec, m...  8.82 us
    dot_general x4, matrix products, per_device(): jnp.einsum('rt,bctp->bcrp', table, moved[m] - mean_field[None, :, None, :...  5.75 us
    ppermute x3, starting transfers between devices, per_device(): moved.append(lax.ppermute(snaps, 'freq', pairs))  4.6 us
    all_to_all x2, waiting for transfers between devices, share(): lax.all_to_all(jnp.broadcast_to(value[None], (size,) + value.shape), axis...  4.46 us
  transfers between devices with their start and end apart: 5, of which 2 were waited for; matrix products, arithmetic and copies ran while one was open for 14% of the time, Pallas kernels for 25%

commit v1 on v0

v1 whole, which is shorter than its diff:
```python
import math

import jax
import jax.numpy as jnp
from jax import lax
from jax.experimental import pallas as pl
from jax.experimental.pallas import tpu as pltpu
from jax.sharding import PartitionSpec as P

EPS = 1e-06


def spectral_table(freq_ids, time_ids, length):
    phase = freq_ids[:, None] * time_ids[None, :] % length
    angle = 2.0 * math.pi / length * phase.astype(jnp.float32)
    window = 0.5 - 0.5 * jnp.cos(2.0 * math.pi / length * time_ids.astype(jnp.float32))
    weight_row = window / math.sqrt(3.0 * length / 8.0)
    return jnp.concatenate(
        (jnp.cos(angle) * weight_row[None], -jnp.sin(angle) * weight_row[None]), axis=0
    )


def split(value):
    high = value.astype(jnp.bfloat16)
    low = (value - high.astype(jnp.float32)).astype(jnp.bfloat16)
    return high, low


def nt_dot(left, right):
    return lax.dot_general(
        left, right, (((1,), (1,)), ((), ())), preferred_element_type=jnp.float32
    )


def rolled(number, one, carry):
    some = math.gcd(number, 4)

    def several(j, carry):
        for i in range(some):
            carry = one(j * some + i, carry)
        return carry

    return lax.fori_loop(0, number // some, several, carry)


def gram_kernel(w_ref, m_ref, g_ref):
    fields = m_ref.shape[2]
    kk = m_ref.shape[3]
    roots = [jnp.sqrt(w_ref[c : c + 1]) for c in range(fields)]

    def one(i, carry):
        total = jnp.zeros((2 * kk, 2 * kk), jnp.float32)
        for c in range(fields):
            both = jnp.concatenate((m_ref[i, 0, c] * roots[c], m_ref[i, 1, c] * roots[c]), axis=0)
            high, low = split(both)
            total += nt_dot(high, high) + nt_dot(low, high) + nt_dot(high, low)
        g_ref[i, :, :kk] = total[:kk, :kk] + total[kk:, kk:]
        g_ref[i, :, kk:] = total[:kk, kk:] - total[kk:, :kk]
        return carry

    rolled(m_ref.shape[0], one, 0)


def lane_sum(value):
    return jnp.sum(value, axis=1, keepdims=True)


def places(number, width):
    me = lax.axis_index("freq")
    return [
        pl.ds(pl.multiple_of(partner_of(me, m, number) * width, width), width)
        for m in range(number)
    ]


def pack_kernel(mean_ref, x_ref, *out_refs):
    width = out_refs[0].shape[3]
    for here, out_ref in zip(places(len(out_refs), width), out_refs):
        for c in range(x_ref.shape[1]):
            out_ref[0, c] = x_ref[0, c, :, here] - mean_ref[c : c + 1, here]


def spectra_kernel(table_ref, *refs):
    number = len(refs) // 2
    in_refs, out_refs = refs[:number], refs[number:]
    th, tl = split(table_ref[...])
    fields = in_refs[0].shape[1]
    _, _, _, count, width = out_refs[0].shape
    for c in range(fields):
        xh, xl = split(jnp.concatenate([ref[0, c] for ref in in_refs], axis=0))
        out = nn_dot(th, xh) + nn_dot(tl, xh) + nn_dot(th, xl)
        out = out.reshape(number, 2, count, width)
        for m in range(number):
            out_refs[m][0, c] = out[m]


def nn_dot(left, right):
    return jnp.dot(left, right, preferred_element_type=jnp.float32)


def project_kernel(w_ref, *refs):
    *q_refs, m_ref, p_ref = refs
    step = pl.program_id(0)
    per_step = m_ref.shape[0]
    fields = m_ref.shape[2]
    kk = m_ref.shape[3]
    count, width = q_refs[0].shape[3:]
    lanes = p_ref.shape[1]

    @pl.when(step == 0)
    def _():
        p_ref[...] = jnp.zeros_like(p_ref)

    lane = lax.broadcasted_iota(jnp.int32, (kk, lanes), 1)
    lane_row = lax.broadcasted_iota(jnp.int32, (1, lanes), 1)
    spots = places(len(q_refs), width)

    def one(i, carry):
        tile, row = carry
        f = step * per_step + i
        accs = [0.0] * 4
        rows = [0.0] * 4
        for here, q_ref in zip(spots, q_refs):
            for c in range(fields):
                mr = m_ref[i, 0, c, :, here]
                mi = m_ref[i, 1, c, :, here]
                w = w_ref[c : c + 1, here]
                qs = [q_ref[b, c, s, pl.ds(f, 1), :] for b in range(2) for s in range(2)]
                wq = [w * q for q in qs]
                for b in range(2):
                    accs[2 * b] += mr * wq[2 * b] + mi * wq[2 * b + 1]
                    accs[2 * b + 1] += mr * wq[2 * b + 1] - mi * wq[2 * b]
                rows[0] += wq[0] * qs[0] + wq[1] * qs[1]
                rows[1] += wq[2] * qs[2] + wq[3] * qs[3]
                rows[2] += wq[0] * qs[2] + wq[1] * qs[3]
                rows[3] += wq[0] * qs[3] - wq[1] * qs[2]
        for j in range(4):
            spot = j * count + f
            tile = jnp.where(lane == spot, lane_sum(accs[j]), tile)
            row = jnp.where(lane_row == spot, lane_sum(rows[j]), row)
        return tile, row

    tile, row = rolled(per_step, one, (p_ref[:kk], p_ref[kk : kk + 1]))
    p_ref[:kk] = tile
    p_ref[kk : kk + 1] = row


def small_math(g_ref, p_ref, rate_ref, coef_ref, tab_ref, point_count):
    kk = g_ref.shape[1]
    count = g_ref.shape[3]
    root = math.sqrt(point_count)
    total = p_ref[...]
    part = [total[:kk, j * count : (j + 1) * count] for j in range(4)]
    row = [total[kk : kk + 1, j * count : (j + 1) * count] for j in range(4)]
    p0r, p0i, p1r, p1i = part
    e00, e11, xr, xi = row
    rate = rate_ref[...]

    def sum_k(value):
        return jnp.sum(value, axis=0, keepdims=True)

    def times_gram(hr, hi):
        vr = jnp.zeros((kk, count), jnp.float32)
        vi = jnp.zeros((kk, count), jnp.float32)
        for l in range(kk):
            gr = g_ref[0, l]
            gi = g_ref[1, l]
            ar = hr[l : l + 1]
            ai = hi[l : l + 1]
            vr += gr * ar - gi * ai
            vi += gr * ai + gi * ar
        return vr, vi

    sub = lax.broadcasted_iota(jnp.int32, (kk, count), 0)
    diag = jnp.zeros((kk, count), jnp.float32)
    for l in range(kk):
        diag = jnp.where(sub == l, g_ref[0, l], diag)

    a0r = p0r / root
    a0i = p0i / root
    gain0 = rate / jnp.sqrt(e00 / point_count + EPS)
    cr = gain0 * a0r
    ci = -gain0 * a0i
    br = a0r / root
    bi = a0i / root
    vr, vi = times_gram(br, bi)
    sr = p0r - vr
    si = p0i - vi
    t0 = e00 - sum_k(br * p0r + bi * p0i) - sum_k(sr * br + si * bi)
    t0 = jnp.maximum(t0, 0.0)
    n0 = diag + 2.0 * (cr * sr - ci * si) + (cr * cr + ci * ci) * t0
    n0 = jnp.maximum(n0, 0.0) / point_count
    d0 = 1.0 / jnp.sqrt(n0 + EPS)
    yr = xr - sum_k(br * p1r + bi * p1i)
    yi = xi - sum_k(br * p1i - bi * p1r)
    u1r = d0 * (p1r + cr * yr + ci * yi)
    u1i = d0 * (p1i + cr * yi - ci * yr)
    a1r = u1r / root
    a1i = u1i / root
    gain1 = rate / jnp.sqrt(e11 / point_count + EPS)
    er = gain1 * a1r
    ei = -gain1 * a1i
    b1r = a1r / root
    b1i = a1i / root
    hr = d0 * b1r
    hi = d0 * b1i
    bigr = sum_k(cr * hr - ci * hi)
    bigi = sum_k(cr * hi + ci * hr)
    zr = sum_k(sr * hr + si * hi)
    zi = sum_k(sr * hi - si * hr)
    vr, vi = times_gram(hr, hi)
    kr = zr + t0 * bigr
    ki = zi + t0 * bigi
    s1r = u1r - d0 * (vr + sr * bigr - si * bigi + cr * kr + ci * ki)
    s1i = u1i - d0 * (vi + sr * bigi + si * bigr + cr * ki - ci * kr)
    t1 = e11 - sum_k(b1r * u1r + b1i * u1i) - sum_k(s1r * b1r + s1i * b1i)
    t1 = jnp.maximum(t1, 0.0)
    n1 = d0 * d0 * n0 * point_count + 2.0 * (er * s1r - ei * s1i) + (er * er + ei * ei) * t1
    n1 = jnp.maximum(n1, 0.0) / point_count
    d1 = 1.0 / jnp.sqrt(n1 + EPS)
    both = d0 * d1
    coef_ref[0, 0] = a0r
    coef_ref[0, 1] = a0i
    coef_ref[1, 0] = a1r
    coef_ref[1, 1] = a1i
    wide = jnp.zeros((kk, count), jnp.float32)
    for n, value in enumerate(
        (br, bi, hr, hi, both, both * cr, both * ci, d1 * er, d1 * ei, wide + bigr, wide + bigi)
    ):
        tab_ref[n] = value


def update_kernel(g_ref, p_ref, rate_ref, *refs, point_count):
    *q_refs, m_ref, out_ref, coef_ref, tab_ref = refs
    step = pl.program_id(0)
    per_step = m_ref.shape[0]
    fields = m_ref.shape[2]
    kk = m_ref.shape[3]
    count, width = q_refs[0].shape[3:]

    @pl.when(step == 0)
    def _():
        small_math(g_ref, p_ref, rate_ref, coef_ref, tab_ref, point_count)

    lane = lax.broadcasted_iota(jnp.int32, (kk, count), 1)

    spots = places(len(q_refs), width)

    def one(i, carry):
        f = step * per_step + i
        here = lane == f
        cols = [lane_sum(jnp.where(here, tab_ref[n], 0.0)) for n in range(tab_ref.shape[0])]
        br, bi, hr, hi, ad, cr, ci, er, ei = [
            jnp.broadcast_to(col, (kk, width)) for col in cols[:9]
        ]
        bigr = cols[9][:1]
        bigi = cols[10][:1]
        for spot, q_ref in zip(spots, q_refs):
            for c in range(fields):
                mr = m_ref[i, 0, c, :, spot]
                mi = m_ref[i, 1, c, :, spot]
                q0r, q0i, q1r, q1i = [
                    q_ref[b, c, s, pl.ds(f, 1), :] for b in range(2) for s in range(2)
                ]
                r0r = q0r - jnp.sum(br * mr - bi * mi, axis=0, keepdims=True)
                r0i = q0i - jnp.sum(br * mi + bi * mr, axis=0, keepdims=True)
                r1r = q1r - jnp.sum(hr * mr - hi * mi, axis=0, keepdims=True)
                r1i = q1i - jnp.sum(hr * mi + hi * mr, axis=0, keepdims=True)
                r1r = r1r - (bigr * r0r - bigi * r0i)
                r1i = r1i - (bigr * r0i + bigi * r0r)
                out_ref[i, 0, c, :, spot] = ad * mr + (cr * r0r - ci * r0i) + (er * r1r - ei * r1i)
                out_ref[i, 1, c, :, spot] = ad * mi + (cr * r0i + ci * r0r) + (er * r1i + ei * r1r)
        return carry

    rolled(per_step, one, 0)


def total_of(value, axis):
    size = lax.axis_size(axis)
    if size & (size - 1):
        wide = jnp.broadcast_to(value[None], (size,) + value.shape)
        return jnp.sum(lax.all_to_all(wide, axis, 0, 0, tiled=True), axis=0)
    hop = 1
    while hop < size:
        value = value + lax.ppermute(value, axis, [(i, i ^ hop) for i in range(size)])
        hop *= 2
    return value


def partner_of(me, m, size):
    return me ^ m if size & (size - 1) == 0 else (m - me) % size


def exchange(parts, axis):
    size = lax.axis_size(axis)
    out = []
    for m, part in enumerate(parts):
        pairs = [(i, partner_of(i, m, size)) for i in range(size)]
        same = all(i == j for i, j in pairs)
        out.append(part if same else lax.ppermute(part, axis, pairs))
    return out


def full(shape):
    return pl.BlockSpec(shape, lambda s: (0,) * len(shape))


def lead(shape):
    return pl.BlockSpec((1,) + shape[1:], lambda s: (s,) + (0,) * (len(shape) - 1))


def per_device(snapshots, mean_field, weights, rates, modes):
    ways = lax.axis_size("freq")
    blocks, quarter, fields, points = snapshots.shape
    assert blocks == 2
    length = quarter * ways
    point_count = fields * points * lax.axis_size("space")
    count, _, kk = modes.shape[:3]
    width = points // ways
    per_step = math.gcd(count, 8)
    steps = count // per_step
    me = lax.axis_index("freq").astype(jnp.int32)
    snaps = snapshots.transpose(0, 2, 1, 3)
    ms = modes.transpose(0, 1, 3, 2, 4)
    partners = jnp.stack([partner_of(me, m, ways) for m in range(ways)]).astype(jnp.int32)

    cut = (blocks, fields, quarter, width)
    parts = pl.pallas_call(
        pack_kernel,
        grid=(blocks,),
        in_specs=[full((fields, points)), lead(snaps.shape)],
        out_specs=[lead(cut)] * ways,
        out_shape=[jax.ShapeDtypeStruct(cut, jnp.float32)] * ways,
        name="pack",
    )(mean_field, snaps)
    parts = exchange(parts, "freq")

    m_spec = pl.BlockSpec((per_step, 2, fields, kk, points), lambda s: (s, 0, 0, 0, 0))
    w_spec = full((fields, points))
    gram = pl.pallas_call(
        gram_kernel,
        grid=(steps,),
        in_specs=[w_spec, m_spec],
        out_specs=pl.BlockSpec((per_step, kk, 2 * kk), lambda s: (s, 0, 0)),
        out_shape=jax.ShapeDtypeStruct((count, kk, 2 * kk), jnp.float32),
        name="gram",
    )(weights, ms)

    freq_ids = partners[:, None] * count + jnp.arange(count, dtype=jnp.int32)[None]
    time_ids = partners[:, None] * quarter + jnp.arange(quarter, dtype=jnp.int32)[None]
    table = spectral_table(freq_ids.reshape(-1), time_ids.reshape(-1), length)
    table = table.reshape(2, ways, count, length).transpose(1, 0, 2, 3)
    table = table.reshape(2 * ways * count, length)
    cut = (blocks, fields, 2, count, width)
    gram, table, *parts = lax.optimization_barrier((gram, table, *parts))
    spectra = pl.pallas_call(
        spectra_kernel,
        grid=(blocks,),
        in_specs=[full(table.shape)] + [lead(parts[0].shape)] * ways,
        out_specs=[lead(cut)] * ways,
        out_shape=[jax.ShapeDtypeStruct(cut, jnp.float32)] * ways,
        name="spectra",
    )(table, *parts)
    spectra = exchange(spectra, "freq")

    gram = total_of(gram.reshape(count * kk * 2 * kk // 128, 128), "space")
    gram = gram.reshape(count, kk, 2, kk).transpose(2, 3, 1, 0)

    rows = -(-(kk + 1) // 8) * 8
    lanes = 4 * count
    q_specs = [full(cut)] * ways
    prods = pl.pallas_call(
        project_kernel,
        grid=(steps,),
        in_specs=[w_spec] + q_specs + [m_spec],
        out_specs=full((rows, lanes)),
        out_shape=jax.ShapeDtypeStruct((rows, lanes), jnp.float32),
        name="project",
    )(weights, *spectra, ms)
    prods = total_of(prods, "space")

    out, coefs = pl.pallas_call(
        lambda *refs: update_kernel(*refs, point_count=point_count),
        grid=(steps,),
        in_specs=[full(gram.shape), full(prods.shape), full((1, count))]
        + q_specs
        + [m_spec],
        out_specs=[m_spec, full((blocks, 2, kk, count))],
        out_shape=[
            jax.ShapeDtypeStruct(ms.shape, jnp.float32),
            jax.ShapeDtypeStruct((blocks, 2, kk, count), jnp.float32),
        ],
        scratch_shapes=[pltpu.VMEM((11, kk, count), jnp.float32)],
        name="update",
    )(gram, prods, rates[None], *spectra, ms)
    return out.transpose(0, 1, 3, 2, 4), coefs.transpose(0, 3, 1, 2)


def solution(mesh):
    return jax.shard_map(
        per_device,
        mesh=mesh,
        in_specs=(
            P(None, "freq", None, "space"),
            P(None, "space"),
            P(None, "space"),
            P("freq"),
            P("freq", None, None, None, "space"),
        ),
        out_specs=(P("freq", None, None, None, "space"), P(None, "freq", None, None)),
        check_vma=False,
    )
```

time: 80.5 us -> 63.3 us (0.79)
  waiting for transfers between devices: 17.5 us -> 9.81 us
  matrix products: 5.75 us -> 0 us
  Pallas kernels: 33.2 us -> 29.8 us
  other arithmetic: 0.51 us -> 2.25 us
  local copies, waits for them, and re-layouts: 6.98 us -> 5.26 us
    ppermute x3 -> x12, starting transfers between devices: 4.6 us -> 15 us  [the longest x6 7.99 us: exchange(): out.append(part if same else lax.ppermute(part, axis, pairs))]
    all_to_all x2 -> x0, starting transfers between devices: 10.3 us -> none  [share(): lax.all_to_all(jnp.broadcast_to(value[None], (size,) + value.shape), axis...]
    dot_general x4 -> x0, matrix products: 5.75 us -> none  [per_device(): jnp.einsum('rt,bctp->bcrp', table, moved[m] - mean_field[None, :, None, :...]
    pallas_call x1, Pallas kernels: 11.4 us -> 6.8 us  [per_device(): pl.pallas_call(gram_kernel, grid=(steps,), in_specs=[w_spec, m_spec], out...]
    broadcast_in_dim x4 -> x0, local copies, waits for them, and re-layouts: 4.54 us -> none  [the longest x3 3.24 us: share(): jnp.broadcast_to(value[None], (size,) + value.shape)]
    all_to_all x2 -> x0, waiting for transfers between devices: 4.46 us -> none  [share(): lax.all_to_all(jnp.broadcast_to(value[None], (size,) + value.shape), axis...]
    ppermute x3 -> x12, waiting for transfers between devices: 13 us -> 9.81 us  [the longest x6 9.16 us: total_of(): lax.ppermute(value, axis, [(i, i ^ hop) for i in range(size)])]
    pallas_call x1 -> x3, Pallas kernels: 8.82 us -> 11.8 us  [the longest x1 6.89 us: per_device(): pl.pallas_call(project_kernel, grid=(steps,), in_specs=[w_spec] + q_specs...]
  transfers between devices with their start and end apart: 5 -> 12, of which waited for: 2 -> 6; matrix products, arithmetic and copies ran while one was open for 14% -> 9% of each run, Pallas kernels for 25% -> 22%
where the time goes in v1:
time: 63.3 us; the launch traced here: 62.9 us
  Pallas kernels  29.8 us (47%)
  starting transfers between devices  15 us (24%)
  waiting for transfers between devices  9.81 us (15%)
  local copies, waits for them, and re-layouts  5.26 us (8%)
  other arithmetic  2.25 us (4%)
  between operations  0.73 us (1%)
    pallas_call x1, Pallas kernels, per_device(): pl.pallas_call(lambda *refs: update_kernel(*refs, point_count=point_count...  11.3 us
    ppermute x6, waiting for transfers between devices, total_of(): lax.ppermute(value, axis, [(i, i ^ hop) for i in range(size)])  9.16 us
    ppermute x6, starting transfers between devices, exchange(): out.append(part if same else lax.ppermute(part, axis, pairs))  7.99 us
    ppermute x6, starting transfers between devices, total_of(): lax.ppermute(value, axis, [(i, i ^ hop) for i in range(size)])  7 us
    pallas_call x1, Pallas kernels, per_device(): pl.pallas_call(project_kernel, grid=(steps,), in_specs=[w_spec] + q_specs...  6.89 us
    pallas_call x1, Pallas kernels, per_device(): pl.pallas_call(gram_kernel, grid=(steps,), in_specs=[w_spec, m_spec], out...  6.8 us
    pallas_call x1, Pallas kernels, per_device(): pl.pallas_call(spectra_kernel, grid=(blocks,), in_specs=[full(table.shape...  2.9 us
    pallas_call x1, Pallas kernels, per_device(): pl.pallas_call(pack_kernel, grid=(blocks,), in_specs=[full((fields, point...  1.99 us
  transfers between devices with their start and end apart: 12, of which 6 were waited for; matrix products, arithmetic and copies ran while one was open for 9% of the time, Pallas kernels for 22%

profile of v1, /device:TPU:0, one launch (start us, length us, event | category | flops | bytes accessed | tf_op | source)
XLA Modules:
  0.0 62.9 jit_solution(10847215881712937768)
XLA Ops:
  0.6 2.0 %pack.1 = (f32[2,3,64,128]{3,2,1,0:T(8,128)}, f32[2,3,64,128]{3,2,1,0:T(8,128)}, f32[2,3,64,128]{3,2,1,0:T(8,128)}, f32[2,3,64,128]{3,2,1,0:T(8,128)}) custom-call(f32[3,512]{1,0:T(4,128)} %mean_ref.1, f32[2,3,64,512]{3,2,1,0:T(8,128)} %bitcast.20), custom_call_target="tpu_custom_call" | custom-call | tf_op jit(solution)/shard_map/pack/pallas_call | solution.py:328
  2.6 3.0 %collective-permute-start = (f32[2,3,64,128]{3,2,1,0:T(8,128)}, f32[2,3,64,128]{3,2,1,0:T(8,128)S(1)}, u32[]{:S(2)}, u32[]{:S(2)}) collective-permute-start(f32[2,3,64,128]{3,2,1,0:T(8,128)} %get-tuple-element.19), channel_id=1, source_target_pairs={{0,8},{8,0},{16,24},{24,16},{1,9},{9,1},{17,25},{25,17},{2,10},{10... | collective-permute-start | bytes 589832 | tf_op jit(solution)/shard_map/ppermute | solution.py:300
  5.6 1.5 %collective-permute-start.1 = (f32[2,3,64,128]{3,2,1,0:T(8,128)}, f32[2,3,64,128]{3,2,1,0:T(8,128)S(1)}, u32[]{:S(2)}, u32[]{:S(2)}) collective-permute-start(f32[2,3,64,128]{3,2,1,0:T(8,128)} %get-tuple-element.20), channel_id=1, source_target_pairs={{0,16},{8,24},{16,0},{24,8},{1,17},{9,25},{17,1},{25,9},{2,18},{10... | collective-permute-start | bytes 589832 | tf_op jit(solution)/shard_map/ppermute | solution.py:300
  7.1 0.0 collective-permute-start.2
  7.1 0.1 broadcast_multiply_fusion.1
  7.2 0.1 iota_add_fusion
  7.3 0.1 add.75
  7.4 0.1 iota_add_fusion.1
  7.5 0.1 add.71
  7.6 0.6 cosine_multiply_fusion
  8.2 0.7 %copy.7 = f32[4,2,32,256]{3,2,1,0:T(8,128)} copy(f32[4,2,32,256]{3,2,0,1:T(8,128)S(1)} %bitcast.18) | data formatting | bytes 524288 | tf_op jit(solution)/shard_map/transpose | solution.py:352
  8.9 6.8 %gram.1 = f32[32,16,32]{2,1,0:T(8,128)} custom-call(f32[3,512]{1,0:T(4,128)} %w_ref.3, f32[32,2,3,16,512]{4,3,2,1,0:T(8,128)} %bitcast.14), custom_call_target="tpu_custom_call" | custom-call | tf_op jit(solution)/shard_map/gram/pallas_call | solution.py:340
  15.7 0.0 collective-permute-done.refs_1_
  15.7 0.6 %collective-permute-done.1.refs_2_ = f32[2,3,64,128]{3,2,1,0:T(8,128)S(1)} collective-permute-done((f32[2,3,64,128]{3,2,1,0:T(8,128)}, f32[2,3,64,128]{3,2,1,0:T(8,128)S(1)}, u32[]{:S(2)}, u32[]{:S(2)}) %collective-permute-start.1) | collective-permute-done | bytes 196640 | tf_op jit(solution)/shard_map/ppermute | solution.py:300
  16.4 0.0 collective-permute-done.2.refs_3_
  16.4 0.0 copy-done.3
  16.4 0.6 %copy-done.4 = f32[2,3,64,128]{3,2,1,0:T(8,128)} copy-done((f32[2,3,64,128]{3,2,1,0:T(8,128)}, f32[2,3,64,128]{3,2,1,0:T(8,128)S(1)}, u32[]{:S(2)}) %copy-start.4) | copy-done | bytes 196632
  17.1 0.1 copy-done.5
  17.1 2.9 %spectra.1 = (f32[2,3,2,32,128]{4,3,2,1,0:T(8,128)}, f32[2,3,2,32,128]{4,3,2,1,0:T(8,128)}, f32[2,3,2,32,128]{4,3,2,1,0:T(8,128)}, f32[2,3,2,32,128]{4,3,2,1,0:T(8,128)}) custom-call(f32[256,256]{1,0:T(8,128)} %bitcast.19, f32[2,3,64,128]{3,2,1,0:T(8,128)} %get-tuple-element.24.refs_0_, f32[2,3,64,128]{3,2,1,0:T(8,128)} %copy-done.3, ...), custom_call_target="tpu_custom_call" | custom-call | tf_op jit(solution)/shard_map/spectra/pallas_call | solution.py:356
  20.0 1.4 %collective-permute-start.6 = (f32[2,3,2,32,128]{4,3,2,1,0:T(8,128)}, f32[2,3,2,32,128]{4,3,2,1,0:T(8,128)S(1)}, u32[]{:S(2)}, u32[]{:S(2)}) collective-permute-start(f32[2,3,2,32,128]{4,3,2,1,0:T(8,128)} %get-tuple-element.29), channel_id=1, source_target_pairs={{0,8},{8,0},{16,24},{24,16},{1,9},{9,1},{17,25},{25,17},{2,10},{10... | collective-permute-start | bytes 589832 | tf_op jit(solution)/shard_map/ppermute | solution.py:300
  21.4 1.5 %collective-permute-start.7 = (f32[2,3,2,32,128]{4,3,2,1,0:T(8,128)}, f32[2,3,2,32,128]{4,3,2,1,0:T(8,128)S(1)}, u32[]{:S(2)}, u32[]{:S(2)}) collective-permute-start(f32[2,3,2,32,128]{4,3,2,1,0:T(8,128)} %get-tuple-element.30), channel_id=1, source_target_pairs={{0,16},{8,24},{16,0},{24,8},{1,17},{9,25},{17,1},{25,9},{2,18},{10... | collective-permute-start | bytes 589832 | tf_op jit(solution)/shard_map/ppermute | solution.py:300
  23.0 0.6 collective-permute-start.8
  23.5 1.1 %reshape.129 = f32[128,128]{1,0:T(8,128)S(1)} reshape(f32[32,16,32]{2,1,0:T(8,128)} %gram.1) | data formatting | bytes 131072 | tf_op jit(solution)/shard_map/reshape | solution.py:366
  24.6 0.1 collective-permute-start.3
  24.7 1.2 %collective-permute-done.3 = f32[128,128]{1,0:T(8,128)S(1)} collective-permute-done((f32[128,128]{1,0:T(8,128)S(1)}, f32[128,128]{1,0:T(8,128)S(1)}, u32[]{:S(2)}, u32[]{:S(2)}) %collective-permute-start.3) | collective-permute-done | bytes 65568 | tf_op jit(solution)/shard_map/ppermute | solution.py:285
  25.9 1.6 %collective-permute-start.4 = (f32[128,128]{1,0:T(8,128)S(1)}, f32[128,128]{1,0:T(8,128)S(1)}, u32[]{:S(2)}, u32[]{:S(2)}) collective-permute-start(f32[128,128]{1,0:T(8,128)S(1)} %add.77), channel_id=1, source_target_pairs={{0,2},{1,3},{2,0},{3,1},{4,6},{5,7},{6,4},{7,5},{8,10},{9,11},{10,... | collective-permute-start | bytes 196616 | tf_op jit(solution)/shard_map/ppermute | solution.py:285
  27.6 2.7 %collective-permute-done.4 = f32[128,128]{1,0:T(8,128)S(1)} collective-permute-done((f32[128,128]{1,0:T(8,128)S(1)}, f32[128,128]{1,0:T(8,128)S(1)}, u32[]{:S(2)}, u32[]{:S(2)}) %collective-permute-start.4) | collective-permute-done | bytes 65568 | tf_op jit(solution)/shard_map/ppermute | solution.py:285
  30.3 2.7 %collective-permute-start.5 = (f32[128,128]{1,0:T(8,128)S(1)}, f32[128,128]{1,0:T(8,128)S(1)}, u32[]{:S(2)}, u32[]{:S(2)}) collective-permute-start(f32[128,128]{1,0:T(8,128)S(1)} %add.78), channel_id=1, source_target_pairs={{0,4},{1,5},{2,6},{3,7},{4,0},{5,1},{6,2},{7,3},{8,12},{9,13},{10,... | collective-permute-start | bytes 196616 | tf_op jit(solution)/shard_map/ppermute | solution.py:285
  32.9 0.0 collective-permute-done.6.refs_1_.refs_4_
  32.9 0.0 collective-permute-done.7.refs_2_.refs_5_
  32.9 0.0 copy-start.1
  32.9 0.0 collective-permute-done.8.refs_3_.refs_6_
  33.0 0.6 %copy-done = f32[2,3,2,32,128]{4,3,2,1,0:T(8,128)} copy-done((f32[2,3,2,32,128]{4,3,2,1,0:T(8,128)}, f32[2,3,2,32,128]{4,3,2,1,0:T(8,128)S(1)}, u32[]{:S(2)}) %copy-start) | copy-done | bytes 196632
  33.6 0.1 copy-done.1
  33.7 0.1 copy-done.2
  33.7 6.9 %project.1 = f32[24,128]{1,0:T(8,128)} custom-call(f32[3,512]{1,0:T(4,128)} %w_ref.3, f32[2,3,2,32,128]{4,3,2,1,0:T(8,128)} %get-tuple-element.28.refs_0_.refs_3_, f32[2,3,2,32,128]{4,3,2,1,0:T(8,128)} %copy-done, f32[2,3,2,32,128]{4,3,2,1,0:T(8,128)} %copy-done.1, f32[2,3,2,32,128]{4,3,2,1,0:T(8,128)} %copy-done.2, f32[32,2,3,16,512]{4,3,2,1,0:T(8,128)} %bitcast.15), custom_call_target="tpu_custom_call" | custom-call | tf_op jit(solution)/shard_map/project/pallas_call | solution.py:372
  40.6 0.0 collective-permute-start.9
  40.6 1.4 %collective-permute-done.9 = f32[24,128]{1,0:T(8,128)S(1)} collective-permute-done((f32[24,128]{1,0:T(8,128)}, f32[24,128]{1,0:T(8,128)S(1)}, u32[]{:S(2)}, u32[]{:S(2)}) %collective-permute-start.9) | collective-permute-done | bytes 12320 | tf_op jit(solution)/shard_map/ppermute | solution.py:285
  42.0 0.7 %add.80 = f32[24,128]{1,0:T(8,128)S(1)} add(f32[24,128]{1,0:T(8,128)} %project.1, f32[24,128]{1,0:T(8,128)S(1)} %collective-permute-done.9) | non-fusion elementwise | flops 3072 | bytes 36864 | tf_op jit(solution)/shard_map/add | solution.py:285
  42.7 1.6 %collective-permute-start.10 = (f32[24,128]{1,0:T(8,128)S(1)}, f32[24,128]{1,0:T(8,128)S(1)}, u32[]{:S(2)}, u32[]{:S(2)}) collective-permute-start(f32[24,128]{1,0:T(8,128)S(1)} %add.80), channel_id=1, source_target_pairs={{0,2},{1,3},{2,0},{3,1},{4,6},{5,7},{6,4},{7,5},{8,10},{9,11},{10,... | collective-permute-start | bytes 36872 | tf_op jit(solution)/shard_map/ppermute | solution.py:285
  44.3 2.1 %collective-permute-done.10 = f32[24,128]{1,0:T(8,128)S(1)} collective-permute-done((f32[24,128]{1,0:T(8,128)S(1)}, f32[24,128]{1,0:T(8,128)S(1)}, u32[]{:S(2)}, u32[]{:S(2)}) %collective-permute-start.10) | collective-permute-done | bytes 12320 | tf_op jit(solution)/shard_map/ppermute | solution.py:285
  46.4 1.1 %collective-permute-start.11 = (f32[24,128]{1,0:T(8,128)S(1)}, f32[24,128]{1,0:T(8,128)S(1)}, u32[]{:S(2)}, u32[]{:S(2)}) collective-permute-start(f32[24,128]{1,0:T(8,128)S(1)} %add.81), channel_id=1, source_target_pairs={{0,4},{1,5},{2,6},{3,7},{4,0},{5,1},{6,2},{7,3},{8,12},{9,13},{10,... | collective-permute-start | bytes 36872 | tf_op jit(solution)/shard_map/ppermute | solution.py:285
  47.5 0.0 collective-permute-done.5
  47.5 0.7 %reshape.130 = f32[32,16,2,16]{3,2,1,0:T(2,128)S(1)} reshape(f32[128,128]{1,0:T(8,128)S(1)} %add.79) | data formatting | bytes 131072 | tf_op jit(solution)/shard_map/reshape | solution.py:367
  48.2 1.1 %copy.8 = f32[32,16,2,16]{0,1,3,2:T(8,128)} copy(f32[32,16,2,16]{3,2,1,0:T(2,128)S(1)} %reshape.130) | data formatting | bytes 131072 | tf_op jit(solution)/shard_map/reshape | solution.py:367
  49.3 1.7 %collective-permute-done.11 = f32[24,128]{1,0:T(8,128)S(1)} collective-permute-done((f32[24,128]{1,0:T(8,128)S(1)}, f32[24,128]{1,0:T(8,128)S(1)}, u32[]{:S(2)}, u32[]{:S(2)}) %collective-permute-start.11) | collective-permute-done | bytes 12320 | tf_op jit(solution)/shard_map/ppermute | solution.py:285
  51.0 0.6 add.82.refs_1_
  51.6 11.3 %update.1 = (f32[32,2,3,16,512]{4,3,2,1,0:T(8,128)}, f32[2,2,16,32]{3,2,1,0:T(8,128)}) custom-call(f32[2,16,16,32]{3,2,1,0:T(8,128)} %bitcast.17, f32[24,128]{1,0:T(8,128)} %add.82.refs_1_, f32[1,32]{1,0:T(1,128)} %bitcast.21, f32[2,3,2,32,128]{4,3,2,1,0:T(8,128)} %get-tuple-element.28.refs_0_.refs_3_, f32[2,3,2,32,128]{4,3,2,1,0:T(8,128)} %copy-done, ...), custom_call_target="tpu_custom_call" | custom-call | tf_op jit(solution)/shard_map/update/pallas_call | solution.py:382
  (12 shorter events, 0.1 us)
Async XLA Ops:
  2.6 13.1 %collective-permute-start = (f32[2,3,64,128]{3,2,1,0:T(8,128)}, f32[2,3,64,128]{3,2,1,0:T(8,128)S(1)}, u32[]{:S(2)}, u32[]{:S(2)}) collective-permute-start(f32[2,3,64,128]{3,2,1,0:T(8,128)} %get-tuple-element.19), channel_id=1, source_target_pairs={{0,8},{8,0},{16,24},{24,16},{1,9},{9,1},{17,25},{25,17},{2,10},{10... | collective-permute-start | bytes 589832 | tf_op jit(solution)/shard_map/ppermute | solution.py:300
  5.6 10.8 %collective-permute-start.1 = (f32[2,3,64,128]{3,2,1,0:T(8,128)}, f32[2,3,64,128]{3,2,1,0:T(8,128)S(1)}, u32[]{:S(2)}, u32[]{:S(2)}) collective-permute-start(f32[2,3,64,128]{3,2,1,0:T(8,128)} %get-tuple-element.20), channel_id=1, source_target_pairs={{0,16},{8,24},{16,0},{24,8},{1,17},{9,25},{17,1},{25,9},{2,18},{10... | collective-permute-start | bytes 589832 | tf_op jit(solution)/shard_map/ppermute | solution.py:300
  7.1 9.3 %collective-permute-start.2 = (f32[2,3,64,128]{3,2,1,0:T(8,128)}, f32[2,3,64,128]{3,2,1,0:T(8,128)S(1)}, u32[]{:S(2)}, u32[]{:S(2)}) collective-permute-start(f32[2,3,64,128]{3,2,1,0:T(8,128)} %get-tuple-element.21), channel_id=1, source_target_pairs={{0,24},{8,16},{16,8},{24,0},{1,25},{9,17},{17,9},{25,1},{2,26},{10... | collective-permute-start | bytes 589832 | tf_op jit(solution)/shard_map/ppermute | solution.py:300
  15.7 0.7 %copy-start.3 = (f32[2,3,64,128]{3,2,1,0:T(8,128)}, f32[2,3,64,128]{3,2,1,0:T(8,128)S(1)}, u32[]{:S(2)}) copy-start(f32[2,3,64,128]{3,2,1,0:T(8,128)S(1)} %collective-permute-done.refs_1_) | copy-start | bytes 589828
  16.4 0.7 %copy-start.4 = (f32[2,3,64,128]{3,2,1,0:T(8,128)}, f32[2,3,64,128]{3,2,1,0:T(8,128)S(1)}, u32[]{:S(2)}) copy-start(f32[2,3,64,128]{3,2,1,0:T(8,128)S(1)} %collective-permute-done.1.refs_2_) | copy-start | bytes 589828
  16.4 0.7 %copy-start.5 = (f32[2,3,64,128]{3,2,1,0:T(8,128)}, f32[2,3,64,128]{3,2,1,0:T(8,128)S(1)}, u32[]{:S(2)}) copy-start(f32[2,3,64,128]{3,2,1,0:T(8,128)S(1)} %collective-permute-done.2.refs_3_) | copy-start | bytes 589828
  20.0 12.9 %collective-permute-start.6 = (f32[2,3,2,32,128]{4,3,2,1,0:T(8,128)}, f32[2,3,2,32,128]{4,3,2,1,0:T(8,128)S(1)}, u32[]{:S(2)}, u32[]{:S(2)}) collective-permute-start(f32[2,3,2,32,128]{4,3,2,1,0:T(8,128)} %get-tuple-element.29), channel_id=1, source_target_pairs={{0,8},{8,0},{16,24},{24,16},{1,9},{9,1},{17,25},{25,17},{2,10},{10... | collective-permute-start | bytes 589832 | tf_op jit(solution)/shard_map/ppermute | solution.py:300
  21.4 11.5 %collective-permute-start.7 = (f32[2,3,2,32,128]{4,3,2,1,0:T(8,128)}, f32[2,3,2,32,128]{4,3,2,1,0:T(8,128)S(1)}, u32[]{:S(2)}, u32[]{:S(2)}) collective-permute-start(f32[2,3,2,32,128]{4,3,2,1,0:T(8,128)} %get-tuple-element.30), channel_id=1, source_target_pairs={{0,16},{8,24},{16,0},{24,8},{1,17},{9,25},{17,1},{25,9},{2,18},{10... | collective-permute-start | bytes 589832 | tf_op jit(solution)/shard_map/ppermute | solution.py:300
  23.0 10.0 %collective-permute-start.8 = (f32[2,3,2,32,128]{4,3,2,1,0:T(8,128)}, f32[2,3,2,32,128]{4,3,2,1,0:T(8,128)S(1)}, u32[]{:S(2)}, u32[]{:S(2)}) collective-permute-start(f32[2,3,2,32,128]{4,3,2,1,0:T(8,128)} %get-tuple-element.31), channel_id=1, source_target_pairs={{0,24},{8,16},{16,8},{24,0},{1,25},{9,17},{17,9},{25,1},{2,26},{10... | collective-permute-start | bytes 589832 | tf_op jit(solution)/shard_map/ppermute | solution.py:300
  24.6 1.3 %collective-permute-start.3 = (f32[128,128]{1,0:T(8,128)S(1)}, f32[128,128]{1,0:T(8,128)S(1)}, u32[]{:S(2)}, u32[]{:S(2)}) collective-permute-start(f32[128,128]{1,0:T(8,128)S(1)} %reshape.129), channel_id=1, source_target_pairs={{0,1},{1,0},{2,3},{3,2},{4,5},{5,4},{6,7},{7,6},{8,9},{9,8},{10,11... | collective-permute-start | bytes 196616 | tf_op jit(solution)/shard_map/ppermute | solution.py:285
  25.9 4.3 %collective-permute-start.4 = (f32[128,128]{1,0:T(8,128)S(1)}, f32[128,128]{1,0:T(8,128)S(1)}, u32[]{:S(2)}, u32[]{:S(2)}) collective-permute-start(f32[128,128]{1,0:T(8,128)S(1)} %add.77), channel_id=1, source_target_pairs={{0,2},{1,3},{2,0},{3,1},{4,6},{5,7},{6,4},{7,5},{8,10},{9,11},{10,... | collective-permute-start | bytes 196616 | tf_op jit(solution)/shard_map/ppermute | solution.py:285
  30.3 17.2 %collective-permute-start.5 = (f32[128,128]{1,0:T(8,128)S(1)}, f32[128,128]{1,0:T(8,128)S(1)}, u32[]{:S(2)}, u32[]{:S(2)}) collective-permute-start(f32[128,128]{1,0:T(8,128)S(1)} %add.78), channel_id=1, source_target_pairs={{0,4},{1,5},{2,6},{3,7},{4,0},{5,1},{6,2},{7,3},{8,12},{9,13},{10,... | collective-permute-start | bytes 196616 | tf_op jit(solution)/shard_map/ppermute | solution.py:285
  32.9 0.7 %copy-start = (f32[2,3,2,32,128]{4,3,2,1,0:T(8,128)}, f32[2,3,2,32,128]{4,3,2,1,0:T(8,128)S(1)}, u32[]{:S(2)}) copy-start(f32[2,3,2,32,128]{4,3,2,1,0:T(8,128)S(1)} %collective-permute-done.6.refs_1_.refs_4_) | copy-start | bytes 589828
  32.9 0.7 %copy-start.1 = (f32[2,3,2,32,128]{4,3,2,1,0:T(8,128)}, f32[2,3,2,32,128]{4,3,2,1,0:T(8,128)S(1)}, u32[]{:S(2)}) copy-start(f32[2,3,2,32,128]{4,3,2,1,0:T(8,128)S(1)} %collective-permute-done.7.refs_2_.refs_5_) | copy-start | bytes 589828
  33.0 0.8 %copy-start.2 = (f32[2,3,2,32,128]{4,3,2,1,0:T(8,128)}, f32[2,3,2,32,128]{4,3,2,1,0:T(8,128)S(1)}, u32[]{:S(2)}) copy-start(f32[2,3,2,32,128]{4,3,2,1,0:T(8,128)S(1)} %collective-permute-done.8.refs_3_.refs_6_) | copy-start | bytes 589828
  40.6 1.4 %collective-permute-start.9 = (f32[24,128]{1,0:T(8,128)}, f32[24,128]{1,0:T(8,128)S(1)}, u32[]{:S(2)}, u32[]{:S(2)}) collective-permute-start(f32[24,128]{1,0:T(8,128)} %project.1), channel_id=1, source_target_pairs={{0,1},{1,0},{2,3},{3,2},{4,5},{5,4},{6,7},{7,6},{8,9},{9,8},{10,11... | collective-permute-start | bytes 36872 | tf_op jit(solution)/shard_map/ppermute | solution.py:285
  42.7 3.7 %collective-permute-start.10 = (f32[24,128]{1,0:T(8,128)S(1)}, f32[24,128]{1,0:T(8,128)S(1)}, u32[]{:S(2)}, u32[]{:S(2)}) collective-permute-start(f32[24,128]{1,0:T(8,128)S(1)} %add.80), channel_id=1, source_target_pairs={{0,2},{1,3},{2,0},{3,1},{4,6},{5,7},{6,4},{7,5},{8,10},{9,11},{10,... | collective-permute-start | bytes 36872 | tf_op jit(solution)/shard_map/ppermute | solution.py:285
  46.4 4.6 %collective-permute-start.11 = (f32[24,128]{1,0:T(8,128)S(1)}, f32[24,128]{1,0:T(8,128)S(1)}, u32[]{:S(2)}, u32[]{:S(2)}) collective-permute-start(f32[24,128]{1,0:T(8,128)S(1)} %add.81), channel_id=1, source_target_pairs={{0,4},{1,5},{2,6},{3,7},{4,0},{5,1},{6,2},{7,3},{8,12},{9,13},{10,... | collective-permute-start | bytes 36872 | tf_op jit(solution)/shard_map/ppermute | solution.py:285
